TPU v7x, 256 devices: a whole 4x4x8 slice. The times are simulated.
256 devices in a mesh: rows: 64 (over z, y, core), cols: 4 (over x).
Axes of the slice: x: 4, y: 4, z: 8, core: 2. Of those that a mesh axis runs over, the one named last changes fastest.
Arguments:
- gradients: float32 [256, 128, 4096], P(None, 'rows', 'cols'), may hold values from -6 to 6
- momentum: float32 [256, 128, 4096], P(None, 'rows', 'cols'), may hold values from -6 to 6
- weights: float32 [256, 128, 4096], P(None, 'rows', 'cols'), may hold values from -0.1875 to 0.1875
Outputs:
- new_weights: float32 [256, 128, 4096], P(None, 'rows', 'cols')
- new_momentum: float32 [256, 128, 4096], P(None, 'rows', 'cols')
All inputs are finite; a program needn't handle non-finite values.
Results may differ from a plain program's by a relative error of at most 0.0003.
Values sent between devices are 32-bit elements.
No kernel may reach another device: no remote copies, remote signals or barrier semaphores. Data moves between devices by JAX's collectives and lax.ppermute only.
A program may use at most 64 MiB of HBM per device.

v0:
```python
import jax
import jax.numpy as jnp
from jax import lax
from jax.sharding import PartitionSpec as P

ITERS = 4


hold_rate = 0.8
learn_rate = 0.8
decay_rate = 0.1


def local(gradients, momentum, weights):
    new_momentum = hold_rate * momentum + gradients
    moved = lax.all_to_all(new_momentum, "rows", split_axis=0, concat_axis=1, tiled=True)
    whole = lax.all_to_all(moved, "cols", split_axis=0, concat_axis=2, tiled=True)
    iterate = whole * lax.rsqrt(jnp.sum(whole * whole, axis=(1, 2), keepdims=True) + 1e-06)
    for step in range(ITERS):
        gram = jnp.einsum("mik,mjk->mij", iterate, iterate, precision=lax.Precision.HIGHEST)
        mixed = -4.775 * gram + 2.0315 * jnp.einsum(
            "mij,mjk->mik", gram, gram, precision=lax.Precision.HIGHEST
        )
        iterate = 3.4445 * iterate + jnp.einsum(
            "mij,mjk->mik", mixed, iterate, precision=lax.Precision.HIGHEST
        )
    iterate = lax.all_to_all(iterate, "cols", split_axis=2, concat_axis=0, tiled=True)
    back = lax.all_to_all(iterate, "rows", split_axis=1, concat_axis=0, tiled=True)
    new_weights = (1.0 - learn_rate * decay_rate) * weights - learn_rate * back
    return (new_weights, new_momentum)


def solution(mesh):
    placed = (P(None, "rows", "cols"), P(None, "rows", "cols"), P(None, "rows", "cols"))
    return jax.shard_map(
        local,
        mesh=mesh,
        in_specs=placed,
        out_specs=(P(None, "rows", "cols"), P(None, "rows", "cols")),
        check_vma=False,
    )
```

profile of v0, /device:TPU:1, one launch (start us, length us, event | category | flops | bytes accessed | tf_op | source)
XLA Modules:
  0.0 228.9 jit_solution(2761105436010172675)
XLA Ops:
  0.6 3.7 %multiply_add_fusion = f32[256,2,1024]{2,1,0:T(2,128)S(1)} fusion(f32[256,2,1024]{2,1,0:T(2,128)} %param.3, f32[256,2,1024]{2,1,0:T(2,128)} %param.4), kind=kLoop, calls=%fused_computation.11 | loop fusion | flops 1048576 | bytes 6291456 | tf_op jit(solution)/shard_map/add | solution.py:15
  4.3 63.3 %all_to_all.54 = f32[256,2,1024]{2,1,0:T(2,128)S(1)} all-to-all(f32[256,2,1024]{2,1,0:T(2,128)S(1)} %multiply_add_fusion), channel_id=1, replica_groups=mesh['rows'=64,'cols'=4] {'rows'}, dimensions={0} | all-to-all | bytes 4194304 | tf_op jit(solution)/shard_map/all_to_all | solution.py:16
  67.6 0.8 copy.32
  68.4 2.4 %all_to_all.43 = f32[4,128,1024]{2,1,0:T(8,128)} reshape(f32[4,64,2,1024]{3,2,1,0:T(2,128)S(1)} %bitcast.56) | data formatting | bytes 4194304 | tf_op jit(solution)/shard_map/all_to_all | solution.py:16
  70.8 28.7 %all_to_all.55 = f32[4,128,1024]{2,1,0:T(8,128)S(1)} all-to-all(f32[4,128,1024]{2,1,0:T(8,128)} %all_to_all.43), channel_id=1, replica_groups=mesh['rows'=64,'cols'=4] {'cols'}, dimensions={0} | all-to-all | bytes 4194304 | tf_op jit(solution)/shard_map/all_to_all | solution.py:17
  99.5 1.1 multiply_reduce_fusion
  101.4 1.8 fusion.4
  103.4 2.6 %multiply_bitcast_fusion.1 = (f32[1,128,4,1024]{3,1,2,0:T(8,128)}, f32[1,128,4,1024]{3,1,2,0:T(8,128)}) fusion(f32[4,128,1024]{2,1,0:T(8,128)S(1)} %all_to_all.55, f32[]{:T(128)S(6)} %rsqrt.4), kind=kLoop, calls=%fused_computation.13 | loop fusion | flops 1048576 | bytes 6291460 | tf_op jit(solution)/shard_map/mul | solution.py:18
  105.9 1.9 copy.26
  107.8 2.9 %copy.25 = f32[1,128,4,1024]{1,3,2,0:T(8,128)} copy(f32[1,128,4,1024]{3,1,2,0:T(8,128)} %get-tuple-element.3) | data formatting | bytes 4194304 | tf_op jit(solution)/shard_map/mul | solution.py:24
  110.7 3.0 %copy.27 = f32[128,4096]{1,0:T(8,128)} copy(f32[128,4096]{0,1:T(8,128)} %bitcast.57) | data formatting | bytes 4194304 | tf_op jit(solution)/shard_map/mul | solution.py:24
  113.7 3.6 %convolution_add_fusion.3 = f32[128,4096]{1,0:T(8,128)S(1)} fusion(f32[128,4096]{1,0:T(8,128)} %copy.27, f32[128,128]{1,0:T(8,128)S(1)} %fusion.10, f32[128,4096]{0,1:T(8,128)S(1)} %bitcast.55), kind=kOutput, calls=%fused_computation.4 | convolution fusion | flops 805830656 | bytes 6356992 | tf_op jit(solution)/shard_map/mij,mjk->mik/dot_general | solution.py:24
  117.3 1.8 fusion.12
  119.3 2.0 convolution_add_fusion.2
  121.3 1.8 fusion.13
  123.3 2.0 convolution_add_fusion.1
  125.4 1.8 fusion.14
  127.4 2.3 fusion
  129.7 3.7 %copy.28 = f32[1,128,4096]{1,0,2:T(1,128)} copy(f32[1,128,4096]{2,1,0:T(8,128)S(1)} %fusion) | data formatting | bytes 4194304 | tf_op jit(solution)/shard_map/add | solution.py:24
  133.4 27.0 %all_to_all.56 = f32[1,128,4096]{1,0,2:T(1,128)S(1)} all-to-all(f32[1,128,4096]{1,0,2:T(1,128)} %copy.28), channel_id=1, replica_groups=mesh['rows'=64,'cols'=4] {'cols'}, dimensions={2} | all-to-all | bytes 4194304 | tf_op jit(solution)/shard_map/all_to_all | solution.py:27
  160.4 2.0 copy.29
  162.3 61.1 %all_to_all.57 = f32[4,128,1024]{2,0,1:T(4,128)S(1)} all-to-all(f32[4,128,1024]{2,0,1:T(4,128)} %bitcast.59), channel_id=1, replica_groups=mesh['rows'=64,'cols'=4] {'rows'}, dimensions={1} | all-to-all | bytes 4194304 | tf_op jit(solution)/shard_map/all_to_all | solution.py:28
  224.0 1.9 copy.30
  226.0 2.9 %bitcast_subtract_fusion = f32[256,2,1024]{2,1,0:T(2,128)} fusion(f32[64,4,2,1024]{3,2,1,0:T(2,128)S(1)} %copy.30, f32[256,2,1024]{2,1,0:T(2,128)S(1)} %copy-done.1), kind=kLoop, calls=%fused_computation.7 | loop fusion | flops 1048576 | bytes 6291456 | tf_op jit(solution)/shard_map/sub | solution.py:29
  (9 shorter events, 1.4 us)
Async XLA Ops:
  4.3 63.3 %copy-start = (f32[256,2,1024]{2,1,0:T(2,128)}, f32[256,2,1024]{2,1,0:T(2,128)S(1)}, u32[]{:S(2)}) copy-start(f32[256,2,1024]{2,1,0:T(2,128)S(1)} %multiply_add_fusion) | copy-start | bytes 6291460
  224.0 2.0 copy-start.1
where the time goes:
time: 230 us; the launch traced here: 229 us
  blocking collectives  180 us (78%)
  local copies, waits for them, and re-layouts  18.6 us (8%)
  matrix products  17.9 us (8%)
  other arithmetic  10.8 us (5%)
    all_to_all x1, blocking collectives, local(): lax.all_to_all(new_momentum, 'rows', split_axis=0, concat_axis=1, tiled=T...  63.3 us
    all_to_all x1, blocking collectives, local(): lax.all_to_all(iterate, 'rows', split_axis=1, concat_axis=0, tiled=True)  61.1 us
    all_to_all x1, blocking collectives, local(): lax.all_to_all(moved, 'cols', split_axis=0, concat_axis=2, tiled=True)  28.7 us
    all_to_all x1, blocking collectives, local(): lax.all_to_all(iterate, 'cols', split_axis=2, concat_axis=0, tiled=True)  27 us
    dot_general x4, matrix products, local(): jnp.einsum('mij,mjk->mik', mixed, iterate, precision=lax.Precision.HIGHEST)  9.94 us
    dot_general x4, matrix products, local(): jnp.einsum('mik,mjk->mij', iterate, iterate, precision=lax.Precision.HIGH...  7.17 us
    mul x2, local copies, waits for them, and re-layouts, local(): 3.4445 * iterate  5.84 us

commit v1 on v0

v1 whole, which is shorter than its diff:
```python
import functools

import jax
import jax.numpy as jnp
from jax import lax
from jax.experimental import pallas as pl
from jax.experimental.pallas import tpu as pltpu
from jax.sharding import PartitionSpec as P

ITERS = 4

hold_rate = 0.8
learn_rate = 0.8
decay_rate = 0.1

LANES = 128
SIDE = 128


def flat(x):
    mats, rows, wide = x.shape
    x = x.reshape(mats, rows, wide // LANES, LANES)
    return x.transpose(0, 2, 1, 3).reshape(-1, LANES)


def unflat(x, shape):
    mats, rows, wide = shape
    x = x.reshape(mats, wide // LANES, rows, LANES)
    return x.transpose(0, 2, 1, 3).reshape(shape)


def split(x):
    high = x.astype(jnp.bfloat16)
    return high, (x - high.astype(jnp.float32)).astype(jnp.bfloat16)


def dot(a, b, dims=((1,), (0,))):
    return lax.dot_general(a, b, (dims, ((), ())), preferred_element_type=jnp.float32)


def dot3(a, b):
    ah, al = split(a)
    bh, bl = split(b)
    return dot(ah, bh) + (dot(ah, bl) + dot(al, bh))


def orthogonal(rows_of, x_ref, y_ref, high_ref, low_ref):
    groups = SIDE // rows_of
    step = x_ref.shape[0] // groups
    tiles = step // rows_of
    for k in range(tiles):
        for r in range(rows_of):
            piece = x_ref[pl.ds(k * rows_of + r, groups, stride=step), :]
            high, low = split(piece)
            at = (slice(r * groups, (r + 1) * groups), slice(k * LANES, (k + 1) * LANES))
            high_ref[at] = high
            low_ref[at] = low
    hh = dot(high_ref[...], high_ref[...], ((1,), (1,)))
    hl = dot(high_ref[...], low_ref[...], ((1,), (1,)))
    gram = hh + (hl + hl.T)
    one = (
        lax.broadcasted_iota(jnp.int32, (SIDE, SIDE), 0)
        == lax.broadcasted_iota(jnp.int32, (SIDE, SIDE), 1)
    ).astype(jnp.float32)
    scale = lax.rsqrt(jnp.sum(gram * one, axis=(0, 1), keepdims=True) + 1e-06)
    gram = gram * scale * scale
    total = None
    for step_ in range(ITERS):
        mixed = 3.4445 * one - 4.775 * gram + 2.0315 * dot3(gram, gram)
        total = mixed if total is None else dot3(mixed, total)
        if step_ < ITERS - 1:
            gram = dot3(mixed, dot3(mixed, gram))
    th, tl = split(total * (learn_rate * scale))
    for k in range(tiles):
        at = (slice(None), slice(k * LANES, (k + 1) * LANES))
        y = dot(th, high_ref[at]) + (dot(th, low_ref[at]) + dot(tl, high_ref[at]))
        for r in range(rows_of):
            y_ref[pl.ds(k * rows_of + r, groups, stride=step), :] = y[r * groups : (r + 1) * groups]


def local(gradients, momentum, weights):
    shape = gradients.shape
    new_momentum = hold_rate * flat(momentum) + flat(gradients)
    axes = ("rows", "cols")
    x = lax.all_to_all(new_momentum, axes, split_axis=0, concat_axis=0, tiled=True)
    wide = x.size // SIDE

    y = pl.pallas_call(
        functools.partial(orthogonal, shape[1]),
        out_shape=jax.ShapeDtypeStruct(x.shape, x.dtype),
        in_specs=[pl.BlockSpec(memory_space=pltpu.VMEM)],
        out_specs=pl.BlockSpec(memory_space=pltpu.VMEM),
        scratch_shapes=[pltpu.VMEM((SIDE, wide), jnp.bfloat16), pltpu.VMEM((SIDE, wide), jnp.bfloat16)],
        name="orthogonal",
    )(x)
    y = lax.all_to_all(y, axes, split_axis=0, concat_axis=0, tiled=True)
    new_weights = (1.0 - learn_rate * decay_rate) * flat(weights) - y
    return (unflat(new_weights, shape), unflat(new_momentum, shape))


def solution(mesh):
    placed = P(None, "rows", "cols")
    return jax.shard_map(
        local,
        mesh=mesh,
        in_specs=(placed, placed, placed),
        out_specs=(placed, placed),
        check_vma=False,
    )
```

time: 230 us -> 153 us (0.67)
  blocking collectives: 180 us -> 68.7 us
  waiting for transfers between devices: 0 us -> 45 us
  matrix products: 17.9 us -> 0 us
  Pallas kernels: 0 us -> 8.62 us
  starting transfers between devices: 0 us -> 6.73 us
  local copies, waits for them, and re-layouts: 18.6 us -> 12.5 us
    all_to_all x4 -> x1, blocking collectives: 180 us -> 68.7 us  [local(): lax.all_to_all(new_momentum, axes, split_axis=0, concat_axis=0, tiled=True)]
    all_to_all x0 -> x1, waiting for transfers between devices: none -> 45 us  [local(): y = lax.all_to_all(y, axes, split_axis=0, concat_axis=0, tiled=True)]
    dot_general x12 -> x0, matrix products: 17.9 us -> none  [the longest x4 9.94 us: local(): jnp.einsum('mij,mjk->mik', mixed, iterate, precision=lax.Precision.HIGHEST)]
    pallas_call x0 -> x1, Pallas kernels: none -> 8.62 us  [local(): pl.pallas_call(functools.partial(orthogonal, shape[1]), out_shape=jax.Sha...]
    all_to_all x0 -> x1, starting transfers between devices: none -> 6.73 us  [local(): y = lax.all_to_all(y, axes, split_axis=0, concat_axis=0, tiled=True)]
    mul x4 -> x1, local copies, waits for them, and re-layouts: 9.68 us -> 3.89 us  [local(): new_weights = (1.0 - learn_rate * decay_rate) * flat(weights) - y]
    all_to_all x3 -> x0, local copies, waits for them, and re-layouts: 5.2 us -> none  [the longest x2 3.24 us: local(): lax.all_to_all(new_momentum, 'rows', split_axis=0, concat_axis=1, tiled=T...]
    reshape x0 -> x1, local copies, waits for them, and re-layouts: none -> 3.24 us  [unflat(): return x.transpose(0, 2, 1, 3).reshape(shape)]
  transfers between devices with their start and end apart: 0 -> 1, of which waited for: 0 -> 1; matrix products, arithmetic and copies ran while one was open for 0% -> 5% of each run, Pallas kernels for 0% -> 0%
where the time goes in v1:
time: 153 us
  blocking collectives  68.7 us (45%)
  waiting for transfers between devices  45 us (29%)
  local copies, waits for them, and re-layouts  12.5 us (8%)
  other arithmetic  10.8 us (7%)
  Pallas kernels  8.62 us (6%)
  starting transfers between devices  6.73 us (4%)
    all_to_all x1, blocking collectives, local(): lax.all_to_all(new_momentum, axes, split_axis=0, concat_axis=0, tiled=True)  68.7 us
    all_to_all x1, waiting for transfers between devices, local(): y = lax.all_to_all(y, axes, split_axis=0, concat_axis=0, tiled=True)  45 us
    pallas_call x1, Pallas kernels, local(): pl.pallas_call(functools.partial(orthogonal, shape[1]), out_shape=jax.Sha...  8.62 us
    all_to_all x1, starting transfers between devices, local(): y = lax.all_to_all(y, axes, split_axis=0, concat_axis=0, tiled=True)  6.73 us
    add x2, local copies, waits for them, and re-layouts, local(): new_momentum = hold_rate * flat(momentum) + flat(gradients)  5.35 us
    mul x1, other arithmetic, local(): new_weights = (1.0 - learn_rate * decay_rate) * flat(weights) - y  3.99 us
    mul x1, local copies, waits for them, and re-layouts, local(): new_weights = (1.0 - learn_rate * decay_rate) * flat(weights) - y  3.89 us
    add x1, other arithmetic, local(): new_momentum = hold_rate * flat(momentum) + flat(gradients)  3.66 us
  transfers between devices with their start and end apart: 1, of which 1 were waited for; matrix products, arithmetic and copies ran while one was open for 5% of the time, Pallas kernels for 0%

profile of v1, /device:TPU:1, one launch (start us, length us, event | category | flops | bytes accessed | tf_op | source)
XLA Modules:
  0.0 152.9 jit_solution(3191481910742166253)
XLA Ops:
  0.6 3.7 %multiply_add_fusion = f32[256,2,1024]{2,1,0:T(2,128)S(1)} fusion(f32[256,2,1024]{2,1,0:T(2,128)} %param.3, f32[256,2,1024]{2,1,0:T(2,128)} %param.4), kind=kLoop, calls=%fused_computation.2 | loop fusion | flops 1048576 | bytes 6291456 | tf_op jit(solution)/shard_map/add | solution.py:83
  4.3 0.0 copy-start
  4.3 2.7 %add.17 = f32[256,2,8,128]{3,2,1,0:T(8,128)} reshape(f32[256,2,1024]{2,1,0:T(2,128)S(1)} %multiply_add_fusion) | data formatting | bytes 4194304 | tf_op jit(solution)/shard_map/add | solution.py:83
  7.0 0.0 copy-done
  7.0 2.7 %copy.5 = f32[256,8,2,128]{3,2,1,0:T(2,128)S(1)} copy(f32[256,8,2,128]{3,1,2,0:T(8,128)} %bitcast.17) | data formatting | bytes 4194304 | tf_op jit(solution)/shard_map/add | solution.py:83
  9.7 68.7 %all_to_all.20 = f32[256,16,128]{2,1,0:T(8,128)} all-to-all(f32[256,16,128]{2,1,0:T(8,128)S(1)} %bitcast.15), channel_id=1, replica_groups=mesh['rows'=64,'cols'=4] {'rows','cols'}, dimensions={0} | all-to-all | bytes 4194304 | tf_op jit(solution)/shard_map/all_to_all | solution.py:85
  78.3 8.6 %orthogonal.1 = f32[4096,128]{1,0:T(8,128)} custom-call(f32[4096,128]{1,0:T(8,128)} %bitcast.16), custom_call_target="tpu_custom_call" | custom-call | tf_op jit(solution)/shard_map/orthogonal/pallas_call | solution.py:88
  86.9 6.7 %all-to-all-start.1 = ((f32[256,16,128]{2,1,0:T(8,128)}), f32[256,16,128]{2,1,0:T(8,128)S(1)}, u32[]{:S(2)}, u32[]{:S(2)}) async-start(f32[256,16,128]{2,1,0:T(8,128)} %bitcast.14), calls=%async_computation.1 | async-start | bytes 4194304 | tf_op jit(solution)/shard_map/all_to_all | solution.py:96
  93.7 4.0 %broadcast_multiply_fusion = f32[256,2,1024]{2,1,0:T(2,128)} fusion(f32[256,2,1024]{2,1,0:T(2,128)} %param.5), kind=kLoop, calls=%fused_computation.3 | loop fusion | flops 524288 | bytes 4194304 | tf_op jit(solution)/shard_map/mul | solution.py:97
  97.7 3.9 %mul.28 = f32[256,2,8,128]{3,2,1,0:T(8,128)} reshape(f32[256,2,1024]{2,1,0:T(2,128)} %broadcast_multiply_fusion) | data formatting | bytes 4194304 | tf_op jit(solution)/shard_map/mul | solution.py:97
  101.6 45.0 %all-to-all-done.1 = f32[256,16,128]{2,1,0:T(8,128)S(1)} async-done(((f32[256,16,128]{2,1,0:T(8,128)}), f32[256,16,128]{2,1,0:T(8,128)S(1)}, u32[]{:S(2)}, u32[]{:S(2)}) %all-to-all-start.1) | async-done | bytes 2097184 | tf_op jit(solution)/shard_map/all_to_all | solution.py:96
  146.5 3.2 %fusion = f32[256,2,8,128]{3,2,1,0:T(8,128)} fusion(f32[256,2,8,128]{3,2,1,0:T(8,128)} %mul.28, f32[256,8,2,128]{3,2,1,0:T(2,128)S(1)} %bitcast.13), kind=kLoop, calls=%fused_computation.1 | loop fusion | flops 524288 | bytes 6291456 | tf_op jit(solution)/shard_map/transpose | solution.py:29
  149.7 3.2 %reshape.31 = f32[256,2,1024]{2,1,0:T(2,128)} reshape(f32[256,2,8,128]{3,2,1,0:T(8,128)} %fusion) | data formatting | bytes 4194304 | tf_op jit(solution)/shard_map/reshape | solution.py:29
Async XLA Ops:
  4.3 2.7 %copy-start = (f32[256,2,1024]{2,1,0:T(2,128)}, f32[256,2,1024]{2,1,0:T(2,128)S(1)}, u32[]{:S(2)}) copy-start(f32[256,2,1024]{2,1,0:T(2,128)S(1)} %multiply_add_fusion) | copy-start | bytes 6291460
  86.9 59.6 %all-to-all-start.1 = ((f32[256,16,128]{2,1,0:T(8,128)}), f32[256,16,128]{2,1,0:T(8,128)S(1)}, u32[]{:S(2)}, u32[]{:S(2)}) async-start(f32[256,16,128]{2,1,0:T(8,128)} %bitcast.14), calls=%async_computation.1 | async-start | bytes 4194304 | tf_op jit(solution)/shard_map/all_to_all | solution.py:96

commit v2 on v1

v2 whole, which is shorter than its diff:
```python
import functools

import jax
import jax.numpy as jnp
from jax import lax
from jax.experimental import pallas as pl
from jax.experimental.layout import Layout, with_layout_constraint
from jax.experimental.pallas import tpu as pltpu
from jax.sharding import PartitionSpec as P

ITERS = 4

hold_rate = 0.8
learn_rate = 0.8
decay_rate = 0.1

LANES = 128
SIDE = 128
CUTS = 4
PAD = 8
ROWS = 512
LIMIT = 24 << 20


def tiled(x):
    return with_layout_constraint(x, Layout(major_to_minor=(0, 2, 1, 3)))


def flat(x):
    mats, rows, wide = x.shape
    x = tiled(x.reshape(mats, rows, wide // LANES, LANES))
    return x.transpose(0, 2, 1, 3).reshape(-1, LANES)


def unflat(x, shape):
    mats, rows, wide = shape
    x = x.reshape(mats, wide // LANES, rows, LANES).transpose(0, 2, 1, 3)
    return tiled(x).reshape(shape)


def split(x):
    high = x.astype(jnp.bfloat16)
    return high, (x - high.astype(jnp.float32)).astype(jnp.bfloat16)


def dot(a, b, dims=((1,), (0,))):
    return lax.dot_general(a, b, (dims, ((), ())), preferred_element_type=jnp.float32)


def dot3(a, b):
    ah, al = split(a)
    bh, bl = split(b)
    return dot(ah, bh) + (dot(ah, bl) + dot(al, bh))


def blend_kernel(momentum_ref, gradients_ref, kept_ref):
    kept_ref[...] = hold_rate * momentum_ref[...] + gradients_ref[...]


def decay_kernel(weights_ref, step_ref, out_ref):
    out_ref[...] = (1.0 - learn_rate * decay_rate) * weights_ref[...] - step_ref[...]


def rowwise(kernel, name, limit, a, *rest):
    block = pl.BlockSpec((ROWS, LANES), lambda i: (i, 0))
    return pl.pallas_call(
        kernel,
        grid=(a.shape[0] // ROWS,),
        out_shape=jax.ShapeDtypeStruct(a.shape, a.dtype),
        in_specs=[block] * (1 + len(rest)),
        out_specs=block,
        cost_estimate=pl.CostEstimate(flops=2 * a.size, bytes_accessed=12 * a.size, transcendentals=0),
        compiler_params=pltpu.CompilerParams(vmem_limit_bytes=limit),
        name=name,
    )(a, *rest)


def orthogonal(rows_of, x_ref, y_ref, in_ref, out_ref, both_ref, in_sem, out_sem):
    groups = SIDE // rows_of
    step = x_ref.shape[0] // groups
    room = step + PAD
    span = step // CUTS
    tiles = span // rows_of

    def cut(ref, rows, i):
        return ref.reshape(groups, rows, LANES).at[:, pl.ds(i * span, span), :]

    def fetch(i):
        return pltpu.make_async_copy(cut(x_ref, step, i), cut(in_ref, room, i), in_sem.at[i])

    def store(i):
        return pltpu.make_async_copy(cut(out_ref, room, i), cut(y_ref, step, i), out_sem.at[i])

    for i in range(CUTS):
        fetch(i).start()
    grams = jnp.zeros((SIDE, 2 * SIDE), jnp.float32)
    for i in range(CUTS):
        fetch(i).wait()
        for k in range(tiles):
            for r in range(rows_of):
                high, low = split(in_ref[pl.ds(i * span + k * rows_of + r, groups, stride=room), :])
                columns = slice((i * tiles + k) * LANES, (i * tiles + k + 1) * LANES)
                both_ref[r * groups : (r + 1) * groups, columns] = high
                both_ref[SIDE + r * groups : SIDE + (r + 1) * groups, columns] = low
        columns = slice(i * tiles * LANES, (i + 1) * tiles * LANES)
        grams += dot(both_ref[:SIDE, columns], both_ref[:, columns], ((1,), (1,)))
    cross = grams[:, SIDE:]
    gram = grams[:, :SIDE] + (cross + cross.T)
    one = (
        lax.broadcasted_iota(jnp.int32, (SIDE, SIDE), 0)
        == lax.broadcasted_iota(jnp.int32, (SIDE, SIDE), 1)
    ).astype(jnp.float32)
    scale = lax.rsqrt(jnp.sum(gram * one, axis=(0, 1), keepdims=True) + 1e-06)
    gram = gram * scale * scale
    total = None
    for turn in range(ITERS):
        mixed = 3.4445 * one - 4.775 * gram + 2.0315 * dot3(gram, gram)
        total = mixed if total is None else dot3(mixed, total)
        if turn < ITERS - 1:
            gram = dot3(mixed, dot3(mixed, gram))
    th, tl = split(total * (learn_rate * scale))
    twice = jnp.concatenate([th, th], axis=1)
    for i in range(CUTS):
        columns = slice(i * tiles * LANES, (i + 1) * tiles * LANES)
        y = dot(twice, both_ref[:, columns]) + dot(tl, both_ref[:SIDE, columns])
        for k in range(tiles):
            for r in range(rows_of):
                where = pl.ds(i * span + k * rows_of + r, groups, stride=room)
                out_ref[where, :] = y[r * groups : (r + 1) * groups, k * LANES : (k + 1) * LANES]
        store(i).start()
    for i in range(CUTS):
        store(i).wait()


def local(gradients, momentum, weights):
    shape = gradients.shape
    new_momentum = rowwise(blend_kernel, "blend", None, flat(momentum), flat(gradients))
    axes = ("rows", "cols")
    x = lax.all_to_all(new_momentum, axes, split_axis=0, concat_axis=0, tiled=True)
    room = x.shape[0] + PAD * SIDE // shape[1]
    y = pl.pallas_call(
        functools.partial(orthogonal, shape[1]),
        out_shape=jax.ShapeDtypeStruct(x.shape, x.dtype),
        in_specs=[pl.BlockSpec(memory_space=pl.ANY)],
        out_specs=pl.BlockSpec(memory_space=pl.ANY),
        scratch_shapes=[
            pltpu.VMEM((room, LANES), jnp.float32),
            pltpu.VMEM((room, LANES), jnp.float32),
            pltpu.VMEM((2 * SIDE, x.size // SIDE), jnp.bfloat16),
            pltpu.SemaphoreType.DMA((CUTS,)),
            pltpu.SemaphoreType.DMA((CUTS,)),
        ],
        name="orthogonal",
    )(x)
    y = lax.all_to_all(y, axes, split_axis=0, concat_axis=0, tiled=True)
    new_weights = rowwise(decay_kernel, "decay", LIMIT, flat(weights), y)
    return (unflat(new_weights, shape), unflat(new_momentum, shape))


def solution(mesh):
    placed = P(None, "rows", "cols")
    return jax.shard_map(
        local,
        mesh=mesh,
        in_specs=(placed, placed, placed),
        out_specs=(placed, placed),
        check_vma=False,
    )
```

time: 153 us -> 145 us (0.948)
  blocking collectives: 68.7 us -> 129 us
  waiting for transfers between devices: 45 us -> 0 us
  local copies, waits for them, and re-layouts: 12.5 us -> 0.01 us
  other arithmetic: 10.8 us -> 0 us
  Pallas kernels: 8.62 us -> 15.8 us
  starting transfers between devices: 6.73 us -> 0 us
    all_to_all x0 -> x1, blocking collectives: none -> 59.7 us  [local(): y = lax.all_to_all(y, axes, split_axis=0, concat_axis=0, tiled=True)]
    all_to_all x1 -> x0, waiting for transfers between devices: 45 us -> none  [local(): y = lax.all_to_all(y, axes, split_axis=0, concat_axis=0, tiled=True)]
    pallas_call x0 -> x2, Pallas kernels: none -> 9.08 us  [rowwise(): pl.pallas_call(kernel, grid=(a.shape[0] // ROWS,), out_shape=jax.ShapeDty...]
    all_to_all x1 -> x0, starting transfers between devices: 6.73 us -> none  [local(): y = lax.all_to_all(y, axes, split_axis=0, concat_axis=0, tiled=True)]
    add x2 -> x0, local copies, waits for them, and re-layouts: 5.35 us -> none  [local(): new_momentum = hold_rate * flat(momentum) + flat(gradients)]
    mul x1 -> x0, other arithmetic: 3.99 us -> none  [local(): new_weights = (1.0 - learn_rate * decay_rate) * flat(weights) - y]
    mul x1 -> x0, local copies, waits for them, and re-layouts: 3.89 us -> none  [local(): new_weights = (1.0 - learn_rate * decay_rate) * flat(weights) - y]
    add x1 -> x0, other arithmetic: 3.66 us -> none  [local(): new_momentum = hold_rate * flat(momentum) + flat(gradients)]
  transfers between devices with their start and end apart: 1 -> 0, of which waited for: 1 -> 0; matrix products, arithmetic and copies ran while one was open for 5% -> 0% of each run, Pallas kernels for 0% -> 0%
where the time goes in v2:
time: 145 us
  blocking collectives  129 us (89%)
  Pallas kernels  15.8 us (11%)
    all_to_all x1, blocking collectives, local(): lax.all_to_all(new_momentum, axes, split_axis=0, concat_axis=0, tiled=True)  68.9 us
    all_to_all x1, blocking collectives, local(): y = lax.all_to_all(y, axes, split_axis=0, concat_axis=0, tiled=True)  59.7 us
    pallas_call x2, Pallas kernels, rowwise(): pl.pallas_call(kernel, grid=(a.shape[0] // ROWS,), out_shape=jax.ShapeDty...  9.08 us
    pallas_call x1, Pallas kernels, local(): pl.pallas_call(functools.partial(orthogonal, shape[1]), out_shape=jax.Sha...  6.67 us

profile of v2, /device:TPU:1, one launch (start us, length us, event | category | flops | bytes accessed | tf_op | source)
XLA Modules:
  0.0 144.9 jit_solution(6637581927017863567)
XLA Ops:
  0.6 6.1 %blend.1 = f32[4096,128]{1,0:T(8,128)} custom-call(f32[4096,128]{1,0:T(8,128)} %bitcast.35, f32[4096,128]{1,0:T(8,128)} %bitcast.36), custom_call_target="tpu_custom_call" | custom-call | flops 1048576 | bytes 6291456 | tf_op jit(solution)/shard_map/blend/pallas_call | solution.py:66
  6.7 68.9 %all_to_all.22 = f32[256,16,128]{2,1,0:T(8,128)} all-to-all(f32[256,16,128]{2,1,0:T(8,128)} %bitcast.31), channel_id=1, replica_groups=mesh['rows'=64,'cols'=4] {'rows','cols'}, dimensions={0} | all-to-all | bytes 4194304 | tf_op jit(solution)/shard_map/all_to_all | solution.py:139
  75.6 6.7 %orthogonal.1 = f32[4096,128]{1,0:T(8,128)} custom-call(f32[4096,128]{1,0:T(8,128)} %bitcast.34), custom_call_target="tpu_custom_call" | custom-call | tf_op jit(solution)/shard_map/orthogonal/pallas_call | solution.py:141
  82.2 0.0 copy-start
  82.2 59.7 %all_to_all.23 = f32[256,16,128]{2,1,0:T(8,128)S(1)} all-to-all(f32[256,16,128]{2,1,0:T(8,128)} %bitcast.33), channel_id=1, replica_groups=mesh['rows'=64,'cols'=4] {'rows','cols'}, dimensions={0} | all-to-all | bytes 4194304 | tf_op jit(solution)/shard_map/all_to_all | solution.py:155
  141.9 0.0 copy-done
  141.9 3.0 %decay.1 = f32[4096,128]{1,0:T(8,128)} custom-call(f32[4096,128]{1,0:T(8,128)S(1)} %bitcast.30, f32[4096,128]{1,0:T(8,128)S(1)} %bitcast.29), custom_call_target="tpu_custom_call" | custom-call | flops 1048576 | bytes 6291456 | tf_op jit(solution)/shard_map/decay/pallas_call | solution.py:66
Async XLA Ops:
  82.2 59.7 %copy-start = (f32[256,2,1024]{2,1,0:T(2,128)S(1)}, f32[256,2,1024]{2,1,0:T(2,128)}, u32[]{:S(2)}) copy-start(f32[256,2,1024]{2,1,0:T(2,128)} %param.5) | copy-start | bytes 6291460

commit v3 on v2

--- a/solution.py
+++ b/solution.py
@@ -18,7 +18,6 @@
 SIDE = 128
 CUTS = 4
 PAD = 8
-ROWS = 512
 LIMIT = 24 << 20
 
 
@@ -53,26 +52,64 @@
     return dot(ah, bh) + (dot(ah, bl) + dot(al, bh))
 
 
-def blend_kernel(momentum_ref, gradients_ref, kept_ref):
-    kept_ref[...] = hold_rate * momentum_ref[...] + gradients_ref[...]
-
-
-def decay_kernel(weights_ref, step_ref, out_ref):
-    out_ref[...] = (1.0 - learn_rate * decay_rate) * weights_ref[...] - step_ref[...]
-
-
-def rowwise(kernel, name, limit, a, *rest):
-    block = pl.BlockSpec((ROWS, LANES), lambda i: (i, 0))
+def blend_kernel(momentum_ref, gradients_ref, out_ref, a_ref, b_ref, c_ref, a_sem, b_sem, c_sem):
+    cut = out_ref.shape[0] // CUTS
+    copies = []
+    for i in range(CUTS):
+        at = pl.ds(i * cut, cut)
+        copies.append(
+            (
+                pltpu.make_async_copy(momentum_ref.at[at], a_ref.at[at], a_sem.at[i]),
+                pltpu.make_async_copy(gradients_ref.at[at], b_ref.at[at], b_sem.at[i]),
+                pltpu.make_async_copy(c_ref.at[at], out_ref.at[at], c_sem.at[i]),
+            )
+        )
+        copies[i][0].start()
+        copies[i][1].start()
+    for i in range(CUTS):
+        copies[i][0].wait()
+        copies[i][1].wait()
+        at = pl.ds(i * cut, cut)
+        c_ref[at] = hold_rate * a_ref[at] + b_ref[at]
+        copies[i][2].start()
+    for i in range(CUTS):
+        copies[i][2].wait()
+
+
+def blend(momentum, gradients):
     return pl.pallas_call(
-        kernel,
-        grid=(a.shape[0] // ROWS,),
-        out_shape=jax.ShapeDtypeStruct(a.shape, a.dtype),
-        in_specs=[block] * (1 + len(rest)),
-        out_specs=block,
-        cost_estimate=pl.CostEstimate(flops=2 * a.size, bytes_accessed=12 * a.size, transcendentals=0),
-        compiler_params=pltpu.CompilerParams(vmem_limit_bytes=limit),
-        name=name,
-    )(a, *rest)
+        blend_kernel,
+        out_shape=jax.ShapeDtypeStruct(momentum.shape, momentum.dtype),
+        in_specs=[pl.BlockSpec(memory_space=pl.ANY)] * 2,
+        out_specs=pl.BlockSpec(memory_space=pl.ANY),
+        scratch_shapes=[pltpu.VMEM(momentum.shape, momentum.dtype)] * 3
+        + [pltpu.SemaphoreType.DMA((CUTS,))] * 3,
+        name="blend",
+    )(momentum, gradients)
+
+
+def decay_kernel(weights_ref, step_ref, out_ref, held_ref, sem):
+    cut = out_ref.shape[0] // CUTS
+    copies = []
+    for i in range(CUTS):
+        at = pl.ds(i * cut, cut)
+        held_ref[at] = (1.0 - learn_rate * decay_rate) * weights_ref[at] - step_ref[at]
+        copies.append(pltpu.make_async_copy(held_ref.at[at], out_ref.at[at], sem.at[i]))
+        copies[i].start()
+    for copy in copies:
+        copy.wait()
+
+
+def decay(weights, step):
+    return pl.pallas_call(
+        decay_kernel,
+        out_shape=jax.ShapeDtypeStruct(weights.shape, weights.dtype),
+        in_specs=[pl.BlockSpec(memory_space=pltpu.VMEM)] * 2,
+        out_specs=pl.BlockSpec(memory_space=pltpu.HBM),
+        scratch_shapes=[pltpu.VMEM(weights.shape, weights.dtype), pltpu.SemaphoreType.DMA((CUTS,))],
+        compiler_params=pltpu.CompilerParams(vmem_limit_bytes=LIMIT),
+        name="decay",
+    )(weights, step)
 
 
 def orthogonal(rows_of, x_ref, y_ref, in_ref, out_ref, both_ref, in_sem, out_sem):
@@ -134,7 +171,7 @@
 
 def local(gradients, momentum, weights):
     shape = gradients.shape
-    new_momentum = rowwise(blend_kernel, "blend", None, flat(momentum), flat(gradients))
+    new_momentum = blend(flat(momentum), flat(gradients))
     axes = ("rows", "cols")
     x = lax.all_to_all(new_momentum, axes, split_axis=0, concat_axis=0, tiled=True)
     room = x.shape[0] + PAD * SIDE // shape[1]
@@ -153,7 +190,7 @@
         name="orthogonal",
     )(x)
     y = lax.all_to_all(y, axes, split_axis=0, concat_axis=0, tiled=True)
-    new_weights = rowwise(decay_kernel, "decay", LIMIT, flat(weights), y)
+    new_weights = decay(flat(weights), y)
     return (unflat(new_weights, shape), unflat(new_momentum, shape))
 
 

time: 145 us -> 141 us (0.972)
  Pallas kernels: 15.8 us -> 11.2 us
    pallas_call x2, Pallas kernels: 9.08 us -> 4.51 us  [the longest x1 3.1 us: blend(): pl.pallas_call(blend_kernel, out_shape=jax.ShapeDtypeStruct(momentum.shap...]
where the time goes in v3:
time: 141 us; the launch traced here: 140 us
  blocking collectives  129 us (91%)
  Pallas kernels  11.2 us (8%)
    all_to_all x1, blocking collectives, local(): lax.all_to_all(new_momentum, axes, split_axis=0, concat_axis=0, tiled=True)  68.9 us
    all_to_all x1, blocking collectives, local(): y = lax.all_to_all(y, axes, split_axis=0, concat_axis=0, tiled=True)  59.7 us
    pallas_call x1, Pallas kernels, local(): pl.pallas_call(functools.partial(orthogonal, shape[1]), out_shape=jax.Sha...  6.67 us
    pallas_call x1, Pallas kernels, blend(): pl.pallas_call(blend_kernel, out_shape=jax.ShapeDtypeStruct(momentum.shap...  3.1 us

profile of v3, /device:TPU:1, one launch (start us, length us, event | category | flops | bytes accessed | tf_op | source)
XLA Modules:
  0.0 140.4 jit_solution(18349842008365810083)
XLA Ops:
  0.6 3.1 %blend.1 = f32[4096,128]{1,0:T(8,128)} custom-call(f32[4096,128]{1,0:T(8,128)} %bitcast.35, f32[4096,128]{1,0:T(8,128)} %bitcast.36), custom_call_target="tpu_custom_call" | custom-call | tf_op jit(solution)/shard_map/blend/pallas_call | solution.py:80
  3.7 68.9 %all_to_all.22 = f32[256,16,128]{2,1,0:T(8,128)} all-to-all(f32[256,16,128]{2,1,0:T(8,128)} %bitcast.31), channel_id=1, replica_groups=mesh['rows'=64,'cols'=4] {'rows','cols'}, dimensions={0} | all-to-all | bytes 4194304 | tf_op jit(solution)/shard_map/all_to_all | solution.py:176
  72.6 6.7 %orthogonal.1 = f32[4096,128]{1,0:T(8,128)} custom-call(f32[4096,128]{1,0:T(8,128)} %bitcast.34), custom_call_target="tpu_custom_call" | custom-call | tf_op jit(solution)/shard_map/orthogonal/pallas_call | solution.py:178
  79.3 0.0 copy-start
  79.3 59.7 %all_to_all.23 = f32[256,16,128]{2,1,0:T(8,128)S(1)} all-to-all(f32[256,16,128]{2,1,0:T(8,128)} %bitcast.33), channel_id=1, replica_groups=mesh['rows'=64,'cols'=4] {'rows','cols'}, dimensions={0} | all-to-all | bytes 4194304 | tf_op jit(solution)/shard_map/all_to_all | solution.py:192
  139.0 0.0 copy-done
  139.0 1.4 %decay.1 = f32[4096,128]{1,0:T(8,128)} custom-call(f32[4096,128]{1,0:T(8,128)S(1)} %bitcast.30, f32[4096,128]{1,0:T(8,128)S(1)} %bitcast.29), custom_call_target="tpu_custom_call" | custom-call | tf_op jit(solution)/shard_map/decay/pallas_call | solution.py:104
Async XLA Ops:
  79.3 59.7 %copy-start = (f32[256,2,1024]{2,1,0:T(2,128)S(1)}, f32[256,2,1024]{2,1,0:T(2,128)}, u32[]{:S(2)}) copy-start(f32[256,2,1024]{2,1,0:T(2,128)} %param.5) | copy-start | bytes 6291460

commit v4 on v3

--- a/solution.py
+++ b/solution.py
@@ -17,7 +17,6 @@
 LANES = 128
 SIDE = 128
 CUTS = 4
-PAD = 8
 LIMIT = 24 << 20
 
 
@@ -112,30 +111,20 @@
     )(weights, step)
 
 
-def orthogonal(rows_of, x_ref, y_ref, in_ref, out_ref, both_ref, in_sem, out_sem):
+def orthogonal(rows_of, wide_of, x_ref, y_ref, both_ref):
     groups = SIDE // rows_of
-    step = x_ref.shape[0] // groups
-    room = step + PAD
-    span = step // CUTS
-    tiles = span // rows_of
+    step = wide_of // LANES * rows_of
+    tiles = wide_of // LANES
+    chunks = x_ref.shape[0] // (groups * step)
 
-    def cut(ref, rows, i):
-        return ref.reshape(groups, rows, LANES).at[:, pl.ds(i * span, span), :]
+    def where(i, k, r):
+        return pl.ds(i * groups * step + k * rows_of + r, groups, stride=step)
 
-    def fetch(i):
-        return pltpu.make_async_copy(cut(x_ref, step, i), cut(in_ref, room, i), in_sem.at[i])
-
-    def store(i):
-        return pltpu.make_async_copy(cut(out_ref, room, i), cut(y_ref, step, i), out_sem.at[i])
-
-    for i in range(CUTS):
-        fetch(i).start()
     grams = jnp.zeros((SIDE, 2 * SIDE), jnp.float32)
-    for i in range(CUTS):
-        fetch(i).wait()
+    for i in range(chunks):
         for k in range(tiles):
             for r in range(rows_of):
-                high, low = split(in_ref[pl.ds(i * span + k * rows_of + r, groups, stride=room), :])
+                high, low = split(x_ref[where(i, k, r), :])
                 columns = slice((i * tiles + k) * LANES, (i * tiles + k + 1) * LANES)
                 both_ref[r * groups : (r + 1) * groups, columns] = high
                 both_ref[SIDE + r * groups : SIDE + (r + 1) * groups, columns] = low
@@ -157,36 +146,26 @@
             gram = dot3(mixed, dot3(mixed, gram))
     th, tl = split(total * (learn_rate * scale))
     twice = jnp.concatenate([th, th], axis=1)
-    for i in range(CUTS):
+    for i in range(chunks):
         columns = slice(i * tiles * LANES, (i + 1) * tiles * LANES)
         y = dot(twice, both_ref[:, columns]) + dot(tl, both_ref[:SIDE, columns])
         for k in range(tiles):
             for r in range(rows_of):
-                where = pl.ds(i * span + k * rows_of + r, groups, stride=room)
-                out_ref[where, :] = y[r * groups : (r + 1) * groups, k * LANES : (k + 1) * LANES]
-        store(i).start()
-    for i in range(CUTS):
-        store(i).wait()
+                y_ref[where(i, k, r), :] = y[r * groups : (r + 1) * groups, k * LANES : (k + 1) * LANES]
 
 
 def local(gradients, momentum, weights):
     shape = gradients.shape
     new_momentum = blend(flat(momentum), flat(gradients))
-    axes = ("rows", "cols")
+    axes = ("cols", "rows")
     x = lax.all_to_all(new_momentum, axes, split_axis=0, concat_axis=0, tiled=True)
-    room = x.shape[0] + PAD * SIDE // shape[1]
     y = pl.pallas_call(
-        functools.partial(orthogonal, shape[1]),
+        functools.partial(orthogonal, shape[1], shape[2]),
         out_shape=jax.ShapeDtypeStruct(x.shape, x.dtype),
-        in_specs=[pl.BlockSpec(memory_space=pl.ANY)],
-        out_specs=pl.BlockSpec(memory_space=pl.ANY),
-        scratch_shapes=[
-            pltpu.VMEM((room, LANES), jnp.float32),
-            pltpu.VMEM((room, LANES), jnp.float32),
-            pltpu.VMEM((2 * SIDE, x.size // SIDE), jnp.bfloat16),
-            pltpu.SemaphoreType.DMA((CUTS,)),
-            pltpu.SemaphoreType.DMA((CUTS,)),
-        ],
+        in_specs=[pl.BlockSpec(memory_space=pltpu.VMEM)],
+        out_specs=pl.BlockSpec(memory_space=pltpu.VMEM),
+        scratch_shapes=[pltpu.VMEM((2 * SIDE, x.size // SIDE), jnp.bfloat16)],
+        compiler_params=pltpu.CompilerParams(vmem_limit_bytes=LIMIT),
         name="orthogonal",
     )(x)
     y = lax.all_to_all(y, axes, split_axis=0, concat_axis=0, tiled=True)

time: 141 us -> 138 us (0.979)
  Pallas kernels: 11.2 us -> 9.13 us
    pallas_call x1, Pallas kernels: 6.67 us -> 4.62 us  [local(): pl.pallas_call(functools.partial(orthogonal, shape[1], shape[2]), out_sha...]
where the time goes in v4:
time: 138 us
  blocking collectives  128 us (93%)
  Pallas kernels  9.13 us (7%)
    all_to_all x1, blocking collectives, local(): lax.all_to_all(new_momentum, axes, split_axis=0, concat_axis=0, tiled=True)  68.3 us
    all_to_all x1, blocking collectives, local(): y = lax.all_to_all(y, axes, split_axis=0, concat_axis=0, tiled=True)  59.9 us
    pallas_call x1, Pallas kernels, local(): pl.pallas_call(functools.partial(orthogonal, shape[1], shape[2]), out_sha...  4.62 us
    pallas_call x1, Pallas kernels, blend(): pl.pallas_call(blend_kernel, out_shape=jax.ShapeDtypeStruct(momentum.shap...  3.11 us

profile of v4, /device:TPU:1, one launch (start us, length us, event | category | flops | bytes accessed | tf_op | source)
XLA Modules:
  0.0 138.0 jit_solution(4110508413463527707)
XLA Ops:
  0.6 3.1 %blend.1 = f32[4096,128]{1,0:T(8,128)} custom-call(f32[4096,128]{1,0:T(8,128)} %bitcast.35, f32[4096,128]{1,0:T(8,128)} %bitcast.36), custom_call_target="tpu_custom_call" | custom-call | tf_op jit(solution)/shard_map/blend/pallas_call | solution.py:79
  3.7 68.3 %all_to_all.22 = f32[256,16,128]{2,1,0:T(8,128)S(1)} all-to-all(f32[256,16,128]{2,1,0:T(8,128)} %bitcast.33), channel_id=1, replica_groups=mesh['rows'=64,'cols'=4] {'cols','rows'}, dimensions={0} | all-to-all | bytes 4194304 | tf_op jit(solution)/shard_map/all_to_all | solution.py:161
  72.0 4.6 %orthogonal.1 = f32[4096,128]{1,0:T(8,128)S(1)} custom-call(f32[4096,128]{1,0:T(8,128)S(1)} %bitcast.31), custom_call_target="tpu_custom_call" | custom-call | tf_op jit(solution)/shard_map/orthogonal/pallas_call | solution.py:162
  76.7 0.0 copy-start
  76.7 59.9 %all_to_all.23 = f32[256,16,128]{2,1,0:T(8,128)S(1)} all-to-all(f32[256,16,128]{2,1,0:T(8,128)S(1)} %bitcast.30), channel_id=1, replica_groups=mesh['rows'=64,'cols'=4] {'cols','rows'}, dimensions={0} | all-to-all | bytes 4194304 | tf_op jit(solution)/shard_map/all_to_all | solution.py:171
  136.6 0.0 copy-done
  136.6 1.4 %decay.1 = f32[4096,128]{1,0:T(8,128)} custom-call(f32[4096,128]{1,0:T(8,128)S(1)} %bitcast.32, f32[4096,128]{1,0:T(8,128)S(1)} %bitcast.29), custom_call_target="tpu_custom_call" | custom-call | tf_op jit(solution)/shard_map/decay/pallas_call | solution.py:103
Async XLA Ops:
  76.7 59.9 %copy-start = (f32[256,2,1024]{2,1,0:T(2,128)S(1)}, f32[256,2,1024]{2,1,0:T(2,128)}, u32[]{:S(2)}) copy-start(f32[256,2,1024]{2,1,0:T(2,128)} %param.5) | copy-start | bytes 6291460

commit v5 on v4

--- a/solution.py
+++ b/solution.py
@@ -17,6 +17,7 @@
 LANES = 128
 SIDE = 128
 CUTS = 4
+PACK = 16
 LIMIT = 24 << 20
 
 
@@ -117,21 +118,23 @@
     tiles = wide_of // LANES
     chunks = x_ref.shape[0] // (groups * step)
 
-    def where(i, k, r):
-        return pl.ds(i * groups * step + k * rows_of + r, groups, stride=step)
-
-    grams = jnp.zeros((SIDE, 2 * SIDE), jnp.float32)
+    gram = jnp.zeros((SIDE, SIDE), jnp.float32)
+    cross = jnp.zeros((SIDE, SIDE), jnp.float32)
     for i in range(chunks):
-        for k in range(tiles):
-            for r in range(rows_of):
-                high, low = split(x_ref[where(i, k, r), :])
+        for g in range(0, groups, PACK):
+            block = x_ref[pl.ds((i * groups + g) * step, PACK * step), :].reshape(PACK, step, LANES)
+            block = jnp.transpose(block, (1, 0, 2))
+            for k in range(tiles):
                 columns = slice((i * tiles + k) * LANES, (i * tiles + k + 1) * LANES)
-                both_ref[r * groups : (r + 1) * groups, columns] = high
-                both_ref[SIDE + r * groups : SIDE + (r + 1) * groups, columns] = low
+                for r in range(rows_of):
+                    high, low = split(block[k * rows_of + r])
+                    row = r * groups + g
+                    both_ref[row : row + PACK, columns] = high
+                    both_ref[SIDE + row : SIDE + row + PACK, columns] = low
         columns = slice(i * tiles * LANES, (i + 1) * tiles * LANES)
-        grams += dot(both_ref[:SIDE, columns], both_ref[:, columns], ((1,), (1,)))
-    cross = grams[:, SIDE:]
-    gram = grams[:, :SIDE] + (cross + cross.T)
+        gram += dot(both_ref[:SIDE, columns], both_ref[:SIDE, columns], ((1,), (1,)))
+        cross += dot(both_ref[:SIDE, columns], both_ref[SIDE:, columns], ((1,), (1,)))
+    gram += cross + cross.T
     one = (
         lax.broadcasted_iota(jnp.int32, (SIDE, SIDE), 0)
         == lax.broadcasted_iota(jnp.int32, (SIDE, SIDE), 1)
@@ -145,13 +148,23 @@
         if turn < ITERS - 1:
             gram = dot3(mixed, dot3(mixed, gram))
     th, tl = split(total * (learn_rate * scale))
-    twice = jnp.concatenate([th, th], axis=1)
+    twice = jnp.concatenate(
+        [jnp.concatenate([th, th], axis=1), jnp.concatenate([tl, jnp.zeros_like(tl)], axis=1)], axis=0
+    )
     for i in range(chunks):
         columns = slice(i * tiles * LANES, (i + 1) * tiles * LANES)
-        y = dot(twice, both_ref[:, columns]) + dot(tl, both_ref[:SIDE, columns])
-        for k in range(tiles):
-            for r in range(rows_of):
-                y_ref[where(i, k, r), :] = y[r * groups : (r + 1) * groups, k * LANES : (k + 1) * LANES]
+        y = dot(twice, both_ref[:, columns])
+        y = y[:SIDE] + y[SIDE:]
+        for g in range(0, groups, PACK):
+            block = jnp.stack(
+                [
+                    y[r * groups + g : r * groups + g + PACK, k * LANES : (k + 1) * LANES]
+                    for k in range(tiles)
+                    for r in range(rows_of)
+                ]
+            )
+            block = jnp.transpose(block, (1, 0, 2)).reshape(PACK * step, LANES)
+            y_ref[pl.ds((i * groups + g) * step, PACK * step), :] = block
 
 
 def local(gradients, momentum, weights):

time: 138 us -> 138 us (level)
  no operation moved by 1% of the time
where the time goes in v5:
time: 138 us
  blocking collectives  128 us (93%)
  Pallas kernels  8.77 us (6%)
    all_to_all x1, blocking collectives, local(): lax.all_to_all(new_momentum, axes, split_axis=0, concat_axis=0, tiled=True)  68.3 us
    all_to_all x1, blocking collectives, local(): y = lax.all_to_all(y, axes, split_axis=0, concat_axis=0, tiled=True)  59.9 us
    pallas_call x1, Pallas kernels, local(): pl.pallas_call(functools.partial(orthogonal, shape[1], shape[2]), out_sha...  4.26 us
    pallas_call x1, Pallas kernels, blend(): pl.pallas_call(blend_kernel, out_shape=jax.ShapeDtypeStruct(momentum.shap...  3.11 us

profile of v5, /device:TPU:1, one launch (start us, length us, event | category | flops | bytes accessed | tf_op | source)
XLA Modules:
  0.0 137.6 jit_solution(14589258830130202524)
XLA Ops:
  0.6 3.1 %blend.1 = f32[4096,128]{1,0:T(8,128)} custom-call(f32[4096,128]{1,0:T(8,128)} %bitcast.35, f32[4096,128]{1,0:T(8,128)} %bitcast.36), custom_call_target="tpu_custom_call" | custom-call | tf_op jit(solution)/shard_map/blend/pallas_call | solution.py:80
  3.7 68.3 %all_to_all.22 = f32[256,16,128]{2,1,0:T(8,128)S(1)} all-to-all(f32[256,16,128]{2,1,0:T(8,128)} %bitcast.33), channel_id=1, replica_groups=mesh['rows'=64,'cols'=4] {'cols','rows'}, dimensions={0} | all-to-all | bytes 4194304 | tf_op jit(solution)/shard_map/all_to_all | solution.py:174
  72.0 4.3 %orthogonal.1 = f32[4096,128]{1,0:T(8,128)S(1)} custom-call(f32[4096,128]{1,0:T(8,128)S(1)} %bitcast.31), custom_call_target="tpu_custom_call" | custom-call | tf_op jit(solution)/shard_map/orthogonal/pallas_call | solution.py:175
  76.3 0.0 copy-start
  76.3 59.9 %all_to_all.23 = f32[256,16,128]{2,1,0:T(8,128)S(1)} all-to-all(f32[256,16,128]{2,1,0:T(8,128)S(1)} %bitcast.30), channel_id=1, replica_groups=mesh['rows'=64,'cols'=4] {'cols','rows'}, dimensions={0} | all-to-all | bytes 4194304 | tf_op jit(solution)/shard_map/all_to_all | solution.py:184
  136.2 0.0 copy-done
  136.2 1.4 %decay.1 = f32[4096,128]{1,0:T(8,128)} custom-call(f32[4096,128]{1,0:T(8,128)S(1)} %bitcast.32, f32[4096,128]{1,0:T(8,128)S(1)} %bitcast.29), custom_call_target="tpu_custom_call" | custom-call | tf_op jit(solution)/shard_map/decay/pallas_call | solution.py:104
Async XLA Ops:
  76.3 59.9 %copy-start = (f32[256,2,1024]{2,1,0:T(2,128)S(1)}, f32[256,2,1024]{2,1,0:T(2,128)}, u32[]{:S(2)}) copy-start(f32[256,2,1024]{2,1,0:T(2,128)} %param.5) | copy-start | bytes 6291460

commit v6 on v5

--- a/solution.py
+++ b/solution.py
@@ -16,7 +16,7 @@
 
 LANES = 128
 SIDE = 128
-CUTS = 4
+CUTS = 8
 PACK = 16
 LIMIT = 24 << 20
 
@@ -122,7 +122,7 @@
     cross = jnp.zeros((SIDE, SIDE), jnp.float32)
     for i in range(chunks):
         for g in range(0, groups, PACK):
-            block = x_ref[pl.ds((i * groups + g) * step, PACK * step), :].reshape(PACK, step, LANES)
+            block = jnp.stack([x_ref[pl.ds(((g + p) * chunks + i) * step, step), :] for p in range(PACK)])
             block = jnp.transpose(block, (1, 0, 2))
             for k in range(tiles):
                 columns = slice((i * tiles + k) * LANES, (i * tiles + k + 1) * LANES)
@@ -163,14 +163,15 @@
                     for r in range(rows_of)
                 ]
             )
-            block = jnp.transpose(block, (1, 0, 2)).reshape(PACK * step, LANES)
-            y_ref[pl.ds((i * groups + g) * step, PACK * step), :] = block
+            block = jnp.transpose(block, (1, 0, 2))
+            for p in range(PACK):
+                y_ref[pl.ds(((g + p) * chunks + i) * step, step), :] = block[p]
 
 
 def local(gradients, momentum, weights):
     shape = gradients.shape
     new_momentum = blend(flat(momentum), flat(gradients))
-    axes = ("cols", "rows")
+    axes = ("rows", "cols")
     x = lax.all_to_all(new_momentum, axes, split_axis=0, concat_axis=0, tiled=True)
     y = pl.pallas_call(
         functools.partial(orthogonal, shape[1], shape[2]),

time: 138 us -> 138 us (level)
  no operation moved by 1% of the time
where the time goes in v6:
time: 138 us
  blocking collectives  129 us (93%)
  Pallas kernels  9.1 us (7%)
    all_to_all x1, blocking collectives, local(): lax.all_to_all(new_momentum, axes, split_axis=0, concat_axis=0, tiled=True)  68.4 us
    all_to_all x1, blocking collectives, local(): y = lax.all_to_all(y, axes, split_axis=0, concat_axis=0, tiled=True)  60.1 us
    pallas_call x1, Pallas kernels, local(): pl.pallas_call(functools.partial(orthogonal, shape[1], shape[2]), out_sha...  4.34 us
    pallas_call x1, Pallas kernels, blend(): pl.pallas_call(blend_kernel, out_shape=jax.ShapeDtypeStruct(momentum.shap...  3.36 us

profile of v6, /device:TPU:1, one launch (start us, length us, event | category | flops | bytes accessed | tf_op | source)
XLA Modules:
  0.0 138.3 jit_solution(15511289593713679816)
XLA Ops:
  0.6 3.4 %blend.1 = f32[4096,128]{1,0:T(8,128)} custom-call(f32[4096,128]{1,0:T(8,128)} %bitcast.35, f32[4096,128]{1,0:T(8,128)} %bitcast.36), custom_call_target="tpu_custom_call" | custom-call | tf_op jit(solution)/shard_map/blend/pallas_call | solution.py:80
  4.0 68.4 %all_to_all.22 = f32[256,16,128]{2,1,0:T(8,128)S(1)} all-to-all(f32[256,16,128]{2,1,0:T(8,128)} %bitcast.33), channel_id=1, replica_groups=mesh['rows'=64,'cols'=4] {'rows','cols'}, dimensions={0} | all-to-all | bytes 4194304 | tf_op jit(solution)/shard_map/all_to_all | solution.py:175
  72.4 4.3 %orthogonal.1 = f32[4096,128]{1,0:T(8,128)S(1)} custom-call(f32[4096,128]{1,0:T(8,128)S(1)} %bitcast.31), custom_call_target="tpu_custom_call" | custom-call | tf_op jit(solution)/shard_map/orthogonal/pallas_call | solution.py:176
  76.8 0.0 copy-start
  76.8 60.1 %all_to_all.23 = f32[256,16,128]{2,1,0:T(8,128)S(1)} all-to-all(f32[256,16,128]{2,1,0:T(8,128)S(1)} %bitcast.30), channel_id=1, replica_groups=mesh['rows'=64,'cols'=4] {'rows','cols'}, dimensions={0} | all-to-all | bytes 4194304 | tf_op jit(solution)/shard_map/all_to_all | solution.py:185
  136.9 0.0 copy-done
  136.9 1.4 %decay.1 = f32[4096,128]{1,0:T(8,128)} custom-call(f32[4096,128]{1,0:T(8,128)S(1)} %bitcast.32, f32[4096,128]{1,0:T(8,128)S(1)} %bitcast.29), custom_call_target="tpu_custom_call" | custom-call | tf_op jit(solution)/shard_map/decay/pallas_call | solution.py:104
Async XLA Ops:
  76.8 60.1 %copy-start = (f32[256,2,1024]{2,1,0:T(2,128)S(1)}, f32[256,2,1024]{2,1,0:T(2,128)}, u32[]{:S(2)}) copy-start(f32[256,2,1024]{2,1,0:T(2,128)} %param.5) | copy-start | bytes 6291460
